TPU v7x, 32 devices: a whole 2x2x4 slice. The times are simulated.
32 devices in a mesh: dp: 4 (over x, y), ep: 8 (over z, core).
Axes of the slice: x: 2, y: 2, z: 4, core: 2. Of those that a mesh axis runs over, the one named last changes fastest.
Arguments:
- x: bfloat16 [4, 8, 256, 3584], P('dp', 'ep'), parts along dimension 0
- expert: int32 [4, 8, 256, 8], P('dp', 'ep'), parts along dimension 0
- slot: int32 [4, 8, 256, 8], P('dp', 'ep'), parts along dimension 0
- gate: float32 [4, 8, 256, 8], P('dp', 'ep'), parts along dimension 0
- w_gate: bfloat16 [32, 3584, 2560], P('ep')
- w_up: bfloat16 [32, 3584, 2560], P('ep')
- w_down: bfloat16 [32, 2560, 3584], P('ep')
- s_gate: bfloat16 [3584, 20480], replicated
- s_up: bfloat16 [3584, 20480], replicated
- s_down: bfloat16 [20480, 3584], replicated
Outputs:
- y: bfloat16 [4, 8, 256, 3584], P('dp', 'ep'), parts along dimension 0
There are 4 independent parts. A program takes and returns all parts, laid end to end along the dimension named above; an argument that names none is the same for every part.
All inputs are finite; a program needn't handle non-finite values.
Results may differ from a plain program's by a relative error of at most 0.009.
Values are sent between devices in bfloat16 or wider.
A program may use at most 2 GiB of HBM per device.

v0:
```python
import jax
import jax.numpy as jnp
from jax import lax
from jax.sharding import NamedSharding, PartitionSpec as P


def einsum(form, a, b):
    return jnp.einsum(form, a.astype(jnp.float32), b.astype(jnp.float32))


def for_all(x, s_gate, s_up, s_down):
    h = jax.nn.silu(einsum("...d,df->...f", x, s_gate)) * einsum("...d,df->...f", x, s_up)
    return einsum("...f,fd->...d", h.astype(jnp.bfloat16), s_down)


def solution(mesh):
    def placed(v, *spec):
        return lax.with_sharding_constraint(v, NamedSharding(mesh, P(*spec)))

    def step(x, expert, slot, gate, w_gate, w_up, w_down, s_gate, s_up, s_down):
        experts, (tokens, top) = w_gate.shape[0], expert.shape[2:]
        slots = 5 * tokens * top // (4 * experts)
        to_expert = jax.nn.one_hot(expert, experts, dtype=jnp.bfloat16)
        to_slot = jax.nn.one_hot(slot, slots, dtype=jnp.bfloat16)
        weighted = to_expert * gate[..., None].astype(jnp.bfloat16)
        dispatch = einsum("abtke,abtkc->abtec", to_expert, to_slot).astype(jnp.bfloat16)
        combine = einsum("abtke,abtkc->abtec", weighted, to_slot).astype(jnp.bfloat16)
        z = einsum("abtec,abtd->aebcd", dispatch, x).astype(jnp.bfloat16)
        z = placed(z, "dp", None, "ep", None, None)
        z = placed(z, "dp", "ep", None, None, None)
        h = jax.nn.silu(einsum("aebcd,edf->aebcf", z, w_gate))
        h = (h * einsum("aebcd,edf->aebcf", z, w_up)).astype(jnp.bfloat16)
        out = einsum("aebcf,efd->aebcd", h, w_down).astype(jnp.bfloat16)
        out = placed(out, "dp", "ep", None, None, None)
        out = placed(out, "dp", None, "ep", None, None)
        y = einsum("abtec,aebcd->abtd", combine, out)
        return (y + for_all(x, s_gate, s_up, s_down)).astype(jnp.bfloat16)

    return step
```

profile of v0, /device:TPU:0, one launch (start us, length us, event | category | flops | bytes accessed | tf_op | source)
XLA Modules:
  0.0 1036.1 jit_solution(15687504399949222441)
XLA Ops:
  0.0 0.0 copy-start
  0.0 1.0 copy.11
  1.0 0.0 copy-start.1
  1.0 0.8 copy.9
  1.8 0.0 copy-start.3
  1.8 3.5 convolution_convert_fusion.2
  5.3 0.0 copy-done
  5.3 12.5 %convolution_convert_fusion = bf16[32,80,3584]{2,1,0:T(8,128)(2,1)} fusion(bf16[256,32,80]{2,1,0:T(8,128)(2,1)} %convolution_convert_fusion.2, bf16[1,1,256,3584]{3,2,1,0:T(8,128)(2,1)S(1)} %copy-done), kind=kOutput, calls=%fused_computation.24 | convolution fusion | flops 4706795520 | bytes 21495808 | tf_op jit(solution)/abtec,abtd->aebcd/dot_general | solution.py:8
  17.8 0.0 copy-done.1
  17.8 0.0 copy-done.3
  17.8 406.3 %all-to-all.4 = bf16[1,8,4,1,80,3584]{5,4,2,3,0,1:T(8,128)(2,1)} all-to-all(bf16[1,8,4,1,80,3584]{5,4,2,3,0,1:T(8,128)(2,1)} %bitcast.143), channel_id=1, replica_groups=mesh['dp'=4,'ep'=8] {'ep'}, dimensions={1} | all-to-all | bytes 36700160 | tf_op jit(solution)/sharding_constraint;jit(solution)/sharding_constraint | solution.py:18
  424.1 59.1 %fusion.2 = f32[4,8,80,2560]{3,2,1,0:T(8,128)} fusion(bf16[4,3584,2560]{2,1,0:T(8,128)(2,1)} %param.5, bf16[1,8,4,1,80,3584]{5,4,2,3,0,1:T(8,128)(2,1)} %all-to-all.4), kind=kOutput, calls=%fused_computation.2 | convolution fusion | flops 46976204800 | bytes 117964800 | tf_op jit(solution)/aebcd,edf->aebcf/dot_general | solution.py:8
  483.2 58.6 %fusion.7 = bf16[1,4,8,80,2560]{4,3,2,1,0:T(8,128)(2,1)} fusion(f32[4,8,80,2560]{3,2,1,0:T(8,128)} %fusion.2, bf16[4,3584,2560]{2,1,0:T(8,128)(2,1)} %param.4, bf16[1,8,4,1,80,3584]{5,4,2,3,0,1:T(8,128)(2,1)} %all-to-all.4), kind=kOutput, calls=%fused_computation.10 | convolution fusion | flops 47015526400 | bytes 131072000 | tf_op jit(solution)/aebcd,edf->aebcf/dot_general | solution.py:8
  541.8 60.1 %convert_bitcast_fusion = bf16[1,4,8,1,80,3584]{5,4,2,1,3,0:T(8,128)(2,1)} fusion(bf16[4,2560,3584]{2,1,0:T(8,128)(2,1)} %param.6, bf16[1,4,8,80,2560]{4,3,2,1,0:T(8,128)(2,1)} %fusion.7), kind=kOutput, calls=%fused_computation.20 | convolution fusion | flops 46985379840 | bytes 104857600 | tf_op jit(solution)/aebcf,efd->aebcd/dot_general | solution.py:8
  601.9 15.7 %copy.15 = bf16[1,4,8,1,80,3584]{5,4,1,3,0,2:T(8,128)(2,1)} copy(bf16[1,4,8,1,80,3584]{5,4,2,1,3,0:T(8,128)(2,1)} %convert_bitcast_fusion) | data formatting | bytes 36700160 | tf_op jit(solution)/sharding_constraint;jit(solution)/sharding_constraint | solution.py:18
  617.6 0.0 copy-start.5
  617.6 0.0 copy-start.2
  617.6 0.0 copy-start.4
  617.6 6.2 all-to-all-start.1
  623.8 0.0 copy-done.5
  623.8 0.1 copy.10
  623.9 0.0 copy-done.2
  623.9 0.0 copy-done.4
  623.9 3.9 convolution_convert_fusion.1
  627.8 63.2 %convolution_bitcast_fusion.1 = f32[1,1,256,20480]{3,2,1,0:T(8,128)} fusion(bf16[3584,20480]{1,0:T(8,128)(2,1)} %param.7, bf16[1,1,256,3584]{3,2,1,0:T(8,128)(2,1)S(1)} %copy-done), kind=kOutput, calls=%fused_computation.7 | convolution fusion | flops 37580963840 | bytes 169607168 | tf_op jit(solution)/...d,df->...f/dot_general | solution.py:8
  691.0 63.2 %fusion.72 = bf16[256,20480]{1,0:T(8,128)(2,1)} fusion(bf16[3584,20480]{1,0:T(8,128)(2,1)} %param.8, bf16[1,1,256,3584]{3,2,1,0:T(8,128)(2,1)S(1)} %copy-done, f32[1,1,256,20480]{3,2,1,0:T(8,128)} %convolution_bitcast_fusion.1), kind=kOutput, calls=%bitcast_fusion.clone.1 | convolution fusion | flops 37612421120 | bytes 180092928 | tf_op jit(solution)/...d,df->...f/dot_general | solution.py:8
  754.2 55.1 %fusion.49 = f32[256,3584]{1,0:T(8,128)} fusion(bf16[20480,3584]{1,0:T(8,128)(2,1)} %param.9, bf16[256,20480]{1,0:T(8,128)(2,1)} %fusion.72), kind=kOutput, calls=%fused_computation.50 | convolution fusion | flops 37580963840 | bytes 160956416 | tf_op jit(solution)/...f,fd->...d/dot_general | solution.py:8
  809.3 211.6 %all-to-all-done.1 = bf16[1,4,8,1,80,3584]{5,4,1,3,0,2:T(8,128)(2,1)} async-done(((bf16[1,4,8,1,80,3584]{5,4,1,3,0,2:T(8,128)(2,1)}), bf16[1,4,8,1,80,3584]{5,4,1,3,0,2:T(8,128)(2,1)}, u32[]{:S(2)}, u32[]{:S(2)}) %all-to-all-start.1) | async-done | bytes 18350112 | tf_op jit(solution)/sharding_constraint;jit(solution)/sharding_constraint | solution.py:18
  1020.9 15.2 %fusion.28 = bf16[1,1,256,3584]{3,2,1,0:T(8,128)(2,1)} fusion(f32[256,3584]{1,0:T(8,128)} %fusion.49, bf16[32,80,3584]{2,1,0:T(8,128)(2,1)} %bitcast.25, bf16[256,32,80]{2,1,0:T(8,128)(2,1)} %convolution_convert_fusion.1), kind=kOutput, calls=%fused_computation.28 | convolution fusion | flops 4699455488 | bytes 25165824 | tf_op jit(solution)/abtec,aebcd->abtd/dot_general | solution.py:8
  (1 shorter events, 0.0 us)
Async XLA Ops:
  0.0 5.3 copy-start
  1.0 16.8 %copy-start.1 = (s32[256,8]{1,0:T(8,128)}, s32[256,8]{1,0:T(8,128)S(1)}, u32[]{:S(2)}) copy-start(s32[256,8]{1,0:T(8,128)S(1)} %copy.11) | copy-start | bytes 24580
  1.8 15.9 %copy-start.3 = (s32[256,8]{1,0:T(8,128)}, s32[256,8]{1,0:T(8,128)S(1)}, u32[]{:S(2)}) copy-start(s32[256,8]{1,0:T(8,128)S(1)} %copy.9) | copy-start | bytes 24580
  617.6 6.2 copy-start.5
  617.6 6.3 copy-start.2
  617.6 6.3 copy-start.4
  617.6 403.3 %all-to-all-start.1 = ((bf16[1,4,8,1,80,3584]{5,4,1,3,0,2:T(8,128)(2,1)}), bf16[1,4,8,1,80,3584]{5,4,1,3,0,2:T(8,128)(2,1)}, u32[]{:S(2)}, u32[]{:S(2)}) async-start(bf16[1,4,8,1,80,3584]{5,4,1,3,0,2:T(8,128)(2,1)} %copy.15), calls=%async_computation.1 | async-start | bytes 36700160 | tf_op jit(solution)/sharding_constraint;jit(solution)/sharding_constraint | solution.py:18
where the time goes:
time: 1040 us
  blocking collectives  406 us (39%)
  matrix products  394 us (38%)
  waiting for transfers between devices  212 us (20%)
  local copies, waits for them, and re-layouts  17.6 us (2%)
    another operation x1, blocking collectives, placed(): return lax.with_sharding_constraint(v, NamedSharding(mesh, P(*spec)))  406 us
    dot_general x10, matrix products, einsum(): return jnp.einsum(form, a.astype(jnp.float32), b.astype(jnp.float32))  394 us
    another operation x1, waiting for transfers between devices, placed(): return lax.with_sharding_constraint(v, NamedSharding(mesh, P(*spec)))  212 us
  transfers between devices with their start and end apart: 1, of which 1 were waited for; matrix products, arithmetic and copies ran while one was open for 18% of the time, Pallas kernels for 0%

commit v1 on v0

v1 whole, which is shorter than its diff:
```python
import functools

import jax
import jax.numpy as jnp
from jax import lax
from jax.experimental import pallas as pl
from jax.experimental.pallas import tpu as pltpu
from jax.sharding import PartitionSpec as P

BF = jnp.bfloat16
F32 = jnp.float32
UP, DOWN = 256, 512
CHUNKS = 2
GROUP = 16
LANES = 128
SIZES = (128, 192, 256, 320, 384)
PARAMS = dict(vmem_limit_bytes=67_043_328)
ANY = pl.BlockSpec(memory_space=pl.ANY)


def dot(a, b):
    return jnp.dot(a, b, preferred_element_type=F32)


def gated(z, wg, wu):
    g = dot(z, wg)
    return (g * jax.nn.sigmoid(g) * dot(z, wu)).astype(BF)


def span(i, size):
    return pl.ds(pl.multiple_of(i * size, size), size)


class Stream:
    def __init__(self, sources, buf, sem, count):
        self.sources, self.buf, self.sem, self.count = sources, buf, sem, count
        self.slots = buf.shape[0]

    def copies(self, i):
        slot = lax.rem(i, self.slots)
        return [
            pltpu.make_async_copy(ref, self.buf.at[slot, k], self.sem.at[slot, k])
            for k, ref in enumerate(self.sources(i))
        ]

    def begin(self):
        for i in range(min(self.slots, self.count)):
            for copy in self.copies(jnp.int32(i)):
                copy.start()

    def take(self, i):
        for copy in self.copies(i):
            copy.wait()
        return self.buf.at[lax.rem(i, self.slots)]

    def free(self, i):
        @pl.when(i + self.slots < self.count)
        def _():
            for copy in self.copies(i + self.slots):
                copy.start()


def shared_kernel(first, groups, ff, x_ref, wg_ref, wu_ref, wd_ref, y_ref, h_ref, ubuf, usem, dbuf, dsem):
    d = x_ref.shape[1]
    ups, downs = ff // UP, d // DOWN

    def up(i):
        at = span(first * ups + i, UP)
        return wg_ref.at[:, at], wu_ref.at[:, at]

    def down(i):
        return (wd_ref.at[span(first + i // downs, ff), span(lax.rem(i, downs), DOWN)],)

    us = Stream(up, ubuf, usem, groups * ups)
    ds = Stream(down, dbuf, dsem, groups * downs)
    us.begin()
    ds.begin()
    y_ref[...] = jnp.zeros_like(y_ref)

    @pl.loop(0, groups)
    def _(g):
        @pl.loop(0, ups)
        def _(s):
            i = g * ups + s
            w = us.take(i)
            h_ref[:, span(s, UP)] = gated(x_ref[...], w[0], w[1])
            us.free(i)

        @pl.loop(0, downs)
        def _(n):
            i = g * downs + n
            w = ds.take(i)
            y_ref[:, span(n, DOWN)] += dot(h_ref[...], w[0])
            ds.free(i)


def shared(x, s_gate, s_up, s_down, ff, first, groups):
    tokens, d = x.shape
    return pl.pallas_call(
        functools.partial(shared_kernel, first, groups, ff),
        in_specs=[pl.BlockSpec(memory_space=pltpu.VMEM)] + [ANY] * 3,
        out_specs=pl.BlockSpec(memory_space=pltpu.VMEM),
        out_shape=jax.ShapeDtypeStruct((tokens, d), F32),
        scratch_shapes=[
            pltpu.VMEM((tokens, ff), BF),
            pltpu.VMEM((4, 2, d, UP), BF),
            pltpu.SemaphoreType.DMA((4, 2)),
            pltpu.VMEM((4, 1, ff, DOWN), BF),
            pltpu.SemaphoreType.DMA((4, 1)),
        ],
        compiler_params=pltpu.CompilerParams(**PARAMS),
        cost_estimate=pl.CostEstimate(
            flops=6 * tokens * d * ff * groups,
            bytes_accessed=6 * d * ff * groups,
            transcendentals=0,
        ),
        name="shared",
    )(x, s_gate, s_up, s_down)


def routed_kernel(experts, x_ref, wg_ref, wu_ref, wd_ref, out_ref, xv, note, rank_ref, col_ref,
                  y_ref, z_ref, h_ref, c_ref, sent, ubuf, usem, dbuf, dsem, xsem, osem):
    mine, d, ff = wg_ref.shape
    tokens = x_ref.shape[0]
    ups, downs = ff // UP, d // DOWN

    def up(i):
        e, at = i // ups, span(lax.rem(i, ups), UP)
        return wg_ref.at[e, :, at], wu_ref.at[e, :, at]

    def down(i):
        return (wd_ref.at[i // downs, :, span(lax.rem(i, downs), DOWN)],)

    def result(n):
        slot = lax.rem(n, 2)
        return pltpu.make_async_copy(sent.at[slot], out_ref.at[:, span(n, DOWN)], osem.at[slot])

    us = Stream(up, ubuf, usem, mine * ups)
    ds = Stream(down, dbuf, dsem, mine * downs)
    note_copy = pltpu.make_async_copy(x_ref.at[:, pl.ds(d, LANES)], note, xsem.at[0])
    x_copy = pltpu.make_async_copy(x_ref.at[:, pl.ds(0, d)], xv, xsem.at[1])
    note_copy.start()
    x_copy.start()
    us.begin()
    ds.begin()
    y_ref[...] = jnp.zeros_like(y_ref)

    me = lax.axis_index("ep") * mine
    k = lax.broadcasted_iota(jnp.int32, (LANES, LANES), 0)
    j = lax.broadcasted_iota(jnp.int32, (LANES, LANES), 1)
    wanted = jnp.where(j < mine, me + j, experts + me + j - mine)
    own = jnp.where((j < 2 * mine) & (k == wanted), 1.0, 0.0).astype(BF)
    note_copy.wait()
    cols = dot(note[...], own)
    before = lax.broadcasted_iota(jnp.int32, (tokens, tokens), 1) <= lax.broadcasted_iota(
        jnp.int32, (tokens, tokens), 0
    )
    upto = dot(jnp.where(before, 1.0, 0.0).astype(BF), cols.astype(BF))
    rank = jnp.where(cols > 0.5, upto - 1.0, -1.0)
    rank_ref[...] = rank.T
    for e in range(mine):
        col_ref[e, :, 0:1] = rank[:, e : e + 1]
        col_ref[e, :, 1:2] = cols[:, mine + e : mine + e + 1]
    x_copy.wait()

    @pl.loop(0, mine)
    def _(e):
        row = rank_ref[pl.ds(e, 1), :]
        count = jnp.max(row).astype(jnp.int32) + 1
        top = SIZES[-1]
        blocks = jnp.where(count > top, 2, 1)
        need = jnp.where(count > top, (count + 1) // 2, count)

        def each(body):
            below = 0
            for m in SIZES:

                @pl.when((need > below) & (need <= m))
                def _():
                    pl.loop(0, blocks)(functools.partial(body, m))

                below = m

        def dispatch(m, b):
            spot = lax.broadcasted_iota(jnp.int32, (m, tokens), 0) + b * m
            pick = jnp.where(row == spot.astype(F32), 1.0, 0.0).astype(BF)

            @pl.loop(0, downs)
            def _(n):
                at = span(n, DOWN)
                z_ref[span(b, m), at] = dot(pick, xv[:, at]).astype(BF)

            spot = lax.broadcasted_iota(jnp.int32, (tokens, m), 1) + b * m
            hit = col_ref[e, :, 0:1] == spot.astype(F32)
            c_ref[b, :, :m] = jnp.where(hit, col_ref[e, :, 1:2], 0.0).astype(BF)

        each(dispatch)

        @pl.loop(0, ups)
        def _(s):
            i = e * ups + s
            w = us.take(i)

            def body(m, b):
                h_ref[span(b, m), span(s, UP)] = gated(z_ref[span(b, m), :], w[0], w[1])

            each(body)
            us.free(i)

        @pl.loop(0, downs)
        def _(n):
            i = e * downs + n
            w = ds.take(i)
            at = span(n, DOWN)

            def body(m, b):
                out = dot(h_ref[span(b, m), :], w[0]).astype(BF)
                y_ref[:, at] += dot(c_ref[b, :, :m], out)

            each(body)
            ds.free(i)

            @pl.when(e == mine - 1)
            def _():
                @pl.when(n >= 2)
                def _():
                    result(n - 2).wait()

                sent[lax.rem(n, 2)] = y_ref[:, at].astype(BF)
                result(n).start()

    for n in range(max(downs - 2, 0), downs):
        result(jnp.int32(n)).wait()


def routed(x, w_gate, w_up, w_down, experts, most):
    tokens, (mine, d, ff) = x.shape[0], w_gate.shape
    top = SIZES[-1]
    rows = 2 * SIZES[-2]
    assert most <= rows
    return pl.pallas_call(
        functools.partial(routed_kernel, experts),
        in_specs=[ANY] * 4,
        out_specs=ANY,
        scratch_shapes=[
            pltpu.VMEM((tokens, d), BF),
            pltpu.VMEM((tokens, LANES), BF),
            pltpu.VMEM((LANES, tokens), F32),
            pltpu.VMEM((mine, tokens, 2), F32),
            pltpu.VMEM((tokens, d), F32),
            pltpu.VMEM((rows, d), BF),
            pltpu.VMEM((rows, ff), BF),
            pltpu.VMEM((2, tokens, top), BF),
            pltpu.VMEM((2, tokens, DOWN), BF),
            pltpu.VMEM((3, 2, d, UP), BF),
            pltpu.SemaphoreType.DMA((3, 2)),
            pltpu.VMEM((2, 1, ff, DOWN), BF),
            pltpu.SemaphoreType.DMA((2, 1)),
            pltpu.SemaphoreType.DMA((2,)),
            pltpu.SemaphoreType.DMA((2,)),
        ],
        out_shape=jax.ShapeDtypeStruct((tokens, d), BF),
        compiler_params=pltpu.CompilerParams(**PARAMS),
        cost_estimate=pl.CostEstimate(
            flops=6 * most * d * ff * mine // 2,
            bytes_accessed=6 * d * ff * mine,
            transcendentals=0,
        ),
        name="routed",
    )(x, w_gate, w_up, w_down)


def solution(mesh):
    members = mesh.shape["ep"]

    def local(x, expert, slot, gate, w_gate, w_up, w_down, s_gate, s_up, s_down):
        x, expert, slot, gate = (v[0, 0] for v in (x, expert, slot, gate))
        (tokens, d), top = x.shape, expert.shape[1]
        mine, _, ff = w_gate.shape
        experts = mine * members
        slots = 5 * tokens * top // (4 * experts)
        part = tokens // CHUNKS
        most = min(members * slots, members * part)

        hit = (expert[:, None, :] == jnp.arange(experts)[None, :, None]) & (slot < slots)[:, None, :]
        weight = gate.astype(BF).astype(F32)[:, None, :]
        note = jnp.concatenate(
            [
                jnp.any(hit, -1).astype(F32),
                jnp.sum(jnp.where(hit, weight, 0.0), -1),
                jnp.zeros((tokens, LANES - 2 * experts), F32),
            ],
            1,
        ).astype(BF)
        deal = jnp.concatenate([x, note], 1).reshape(part // GROUP, CHUNKS, GROUP, d + LANES)
        xs = [deal[:, c].reshape(part, d + LANES) for c in range(CHUNKS)]
        xs = [lax.all_gather(v, "ep").reshape(members * part, d + LANES) for v in xs]

        half = s_gate.shape[1] // ff // 2
        rest = s_gate.shape[1] // ff - half
        sh = shared(x, s_gate, s_up, s_down, ff, 0, half)
        (sh, xs[0]) = lax.optimization_barrier((sh, xs[0]))
        sums = []
        for c in range(CHUNKS):
            y = routed(xs[c], w_gate, w_up, w_down, experts, most)
            if c + 1 < CHUNKS:
                y, xs[c + 1] = lax.optimization_barrier((y, xs[c + 1]))
            else:
                y, x = lax.optimization_barrier((y, x))
            sums.append(lax.psum_scatter(y.reshape(members, part, d), "ep"))
        sh2 = shared(x, s_gate, s_up, s_down, ff, half, rest)
        y = jnp.stack([v.reshape(part // GROUP, GROUP, d) for v in sums], 1).reshape(tokens, d)
        y = y.astype(F32) + (sh + sh2)
        return y.astype(BF)[None, None]

    held = P("dp", "ep", None, None)
    split, whole = P("ep", None, None), P(None, None)
    return jax.shard_map(
        local,
        mesh=mesh,
        in_specs=(held,) * 4 + (split,) * 3 + (whole,) * 3,
        out_specs=held,
        check_vma=False,
    )
```

time: 1040 us -> 529 us (0.51)
  Pallas kernels: 0 us -> 413 us
  blocking collectives: 406 us -> 0 us
  matrix products: 394 us -> 0 us
  waiting for transfers between devices: 212 us -> 86.9 us
  between operations: 0.08 us -> 13.2 us
    pallas_call x0 -> x4, Pallas kernels: none -> 413 us  [the longest x2 256 us: routed(): pl.pallas_call(functools.partial(routed_kernel, experts), in_specs=[ANY]...]
    another operation x1 -> x0, blocking collectives: 406 us -> none  [placed(): return lax.with_sharding_constraint(v, NamedSharding(mesh, P(*spec)))]
    dot_general x10 -> x0, matrix products: 394 us -> none  [einsum(): return jnp.einsum(form, a.astype(jnp.float32), b.astype(jnp.float32))]
    another operation x1 -> x0, waiting for transfers between devices: 212 us -> none  [placed(): return lax.with_sharding_constraint(v, NamedSharding(mesh, P(*spec)))]
    reduce_scatter x0 -> x2, waiting for transfers between devices: none -> 85.6 us  [local(): sums.append(lax.psum_scatter(y.reshape(members, part, d), 'ep'))]
    another operation x1 -> x3, local copies, waits for them, and re-layouts: 15.7 us -> 0.24 us  [placed(): return lax.with_sharding_constraint(v, NamedSharding(mesh, P(*spec)))]
  transfers between devices with their start and end apart: 1 -> 4, of which waited for: 1 -> 2; matrix products, arithmetic and copies ran while one was open for 18% -> 0% of each run, Pallas kernels for 0% -> 53%
where the time goes in v1:
time: 529 us; the launch traced here: 528 us
  Pallas kernels  413 us (78%)
  waiting for transfers between devices  86.9 us (16%)
  between operations  13.2 us (2%)
  local copies, waits for them, and re-layouts  7.81 us (1%)
  other arithmetic  6.19 us (1%)
    pallas_call x2, Pallas kernels, routed(): pl.pallas_call(functools.partial(routed_kernel, experts), in_specs=[ANY]...  256 us
    pallas_call x2, Pallas kernels, shared(): pl.pallas_call(functools.partial(shared_kernel, first, groups, ff), in_sp...  158 us
    reduce_scatter x2, waiting for transfers between devices, local(): sums.append(lax.psum_scatter(y.reshape(members, part, d), 'ep'))  85.6 us
  transfers between devices with their start and end apart: 4, of which 2 were waited for; matrix products, arithmetic and copies ran while one was open for 0% of the time, Pallas kernels for 53%

profile of v1, /device:TPU:0, one launch (start us, length us, event | category | flops | bytes accessed | tf_op | source)
XLA Modules:
  0.0 527.7 jit_solution(3442662667586921832)
XLA Ops:
  6.5 0.0 copy-start.2
  6.5 0.0 copy-start.1
  6.5 0.0 copy-start.3
  6.5 0.0 all-gather.3.cloned.1.call-start
  6.5 2.9 copy.26
  9.4 0.0 copy-done.2
  9.4 0.0 copy-done.1
  9.4 0.1 fusion.3
  9.6 0.1 copy.24
  9.7 0.0 copy-done.3
  9.7 0.1 select_reduce_fusion
  9.8 0.1 copy.25
  10.0 2.4 concatenate.14
  12.4 1.4 fusion.4
  13.8 0.0 all-gather.3.cloned.1.call-update
  13.8 0.0 all-gather.5.cloned.1.call-start
  13.9 0.7 all-gather.5.cloned.1.call-update
  14.6 0.0 reduce-scatter.5.cloned.1.call-start
  14.6 79.1 %shared.2 = f32[256,3584]{1,0:T(8,128)} custom-call(bf16[256,3584]{1,0:T(8,128)(2,1)} %bitcast.24, bf16[3584,20480]{1,0:T(8,128)(2,1)} %wg_ref.7, bf16[3584,20480]{1,0:T(8,128)(2,1)} %wu_ref.7, bf16[20480,3584]{1,0:T(8,128)(2,1)} %wd_ref.7), custom_call_target="tpu_custom_call" | custom-call | flops 56371445760 | bytes 220200960 | tf_op jit(solution)/shard_map/shared/pallas_call | solution.py:99
  93.8 0.0 all-gather.3.cloned.1.call-done
  93.8 122.9 %routed.2 = bf16[1024,3584]{1,0:T(8,128)(2,1)} custom-call(bf16[1024,3712]{1,0:T(8,128)(2,1)} %bitcast.36, bf16[4,3584,2560]{2,1,0:T(8,128)(2,1)} %wg_ref.6, bf16[4,3584,2560]{2,1,0:T(8,128)(2,1)} %wu_ref.6, bf16[4,2560,3584]{2,1,0:T(8,128)(2,1)} %wd_ref.6), custom_call_target="tpu_custom_call" | custom-call | flops 70464307200 | bytes 220200960 | tf_op jit(solution)/shard_map/routed/pallas_call | solution.py:241
  216.7 0.0 all-gather.5.cloned.1.call-done
  216.8 132.9 %routed.3 = bf16[1024,3584]{1,0:T(8,128)(2,1)} custom-call(bf16[1024,3712]{1,0:T(8,128)(2,1)} %bitcast.37, bf16[4,3584,2560]{2,1,0:T(8,128)(2,1)} %wg_ref.6, bf16[4,3584,2560]{2,1,0:T(8,128)(2,1)} %wu_ref.6, bf16[4,2560,3584]{2,1,0:T(8,128)(2,1)} %wd_ref.6), custom_call_target="tpu_custom_call" | custom-call | flops 70464307200 | bytes 220200960 | tf_op jit(solution)/shard_map/routed/pallas_call | solution.py:241
  349.7 0.0 reduce-scatter.5.cloned.1.call-update
  349.7 0.0 reduce-scatter.3.cloned.1.call-start
  349.8 0.5 reduce-scatter.3.cloned.1.call-update
  350.3 78.4 %shared.3 = f32[256,3584]{1,0:T(8,128)} custom-call(bf16[256,3584]{1,0:T(8,128)(2,1)} %bitcast.25, bf16[3584,20480]{1,0:T(8,128)(2,1)} %wg_ref.7, bf16[3584,20480]{1,0:T(8,128)(2,1)} %wu_ref.7, bf16[20480,3584]{1,0:T(8,128)(2,1)} %wd_ref.7), custom_call_target="tpu_custom_call" | custom-call | flops 56371445760 | bytes 220200960 | tf_op jit(solution)/shard_map/shared/pallas_call | solution.py:99
  428.7 5.3 %reduce-scatter.5.cloned.1.call-done = bf16[1,128,3584]{2,1,0:T(8,128)(2,1)} async-done(((bf16[8,128,3584]{2,1,0:T(8,128)(2,1)}), bf16[1,128,3584]{2,1,0:T(8,128)(2,1)}) %reduce-scatter.5.cloned.1.call-update) | async-done | bytes 917520 | tf_op jit(solution)/shard_map/reduce_scatter | solution.py:310
  434.0 80.3 %reduce-scatter.3.cloned.1.call-done = bf16[1,128,3584]{2,1,0:T(8,128)(2,1)} async-done(((bf16[8,128,3584]{2,1,0:T(8,128)(2,1)}), bf16[1,128,3584]{2,1,0:T(8,128)(2,1)}) %reduce-scatter.3.cloned.1.call-update) | async-done | bytes 917520 | tf_op jit(solution)/shard_map/reduce_scatter | solution.py:310
  514.4 0.0 copy-start
  514.4 1.8 pad_maximum_fusion
  516.1 0.8 copy-done
  516.9 4.2 fusion.1
  (6 shorter events, 0.0 us)
Async XLA Ops:
  6.5 2.9 copy-start.2
  6.5 2.9 copy-start.1
  6.5 3.1 copy-start.3
  6.5 87.3 %all-gather.3.cloned.1.call-start = ((), (), s32[]{:S(2)}) async-start(), calls=%async_computation.2 | async-start | bytes 8552448 | tf_op jit(solution)/shard_map/all_gather | solution.py:297
  13.8 202.9 %all-gather.5.cloned.1.call-start = ((), (), s32[]{:S(2)}) async-start(), calls=%async_computation.3 | async-start | bytes 8552448 | tf_op jit(solution)/shard_map/all_gather | solution.py:297
  14.6 419.4 %reduce-scatter.5.cloned.1.call-start = ((), (), s32[]{:S(2)}) async-start(), calls=%async_computation.5 | async-start | bytes 8257536 | tf_op jit(solution)/shard_map/reduce_scatter | solution.py:310
  349.7 164.7 %reduce-scatter.3.cloned.1.call-start = ((), (), s32[]{:S(2)}) async-start(), calls=%async_computation.4 | async-start | bytes 8257536 | tf_op jit(solution)/shard_map/reduce_scatter | solution.py:310
  514.4 2.6 copy-start
Sparse Core Ops, SparseCore 0:
  14.0 78.2 all-gather.2
  93.9 74.0 all-gather.4
  349.8 84.1 reduce-scatter.4
  436.2 78.1 reduce-scatter.2
